TPU v7x, 128 devices: a whole 4x4x4 slice. The times are simulated.
128 devices in a mesh: ep: 32 (over y, z, core), dp: 4 (over x).
Axes of the slice: x: 4, y: 4, z: 4, core: 2. Of those that a mesh axis runs over, the one named last changes fastest.
Arguments:
- tokens_q: bfloat16 [8192, 3584], P(('dp', 'ep')), parts along dimension 0, may hold values from -448 to 448
- token_scale: float32 [8192, 28], P(('dp', 'ep')), parts along dimension 0, may hold values from 0.003 to 0.03
- residual: bfloat16 [8192, 3584], P(('dp', 'ep')), parts along dimension 0, may hold values from -6 to 6
- expert_ids: int32 [8192, 8], P(('dp', 'ep')), parts along dimension 0, may hold values from 0 to 31, all different within a row; in each aligned block of 64 rows (0 to 63, 64 to 127, ...) at most 32 rows name the same one
- gate_values: float32 [8192, 8], P(('dp', 'ep')), parts along dimension 0, may hold values from 0.1 to 1
- w_gate: bfloat16 [32, 3584, 1024], P('ep'), may hold values from -0.09375 to 0.09375
- w_up: bfloat16 [32, 3584, 1024], P('ep'), may hold values from -0.09375 to 0.09375
- w_down: bfloat16 [32, 1024, 3584], P('ep'), may hold values from -0.1875 to 0.1875
- norm_gain: float32 [3584], replicated, may hold values from 0.5 to 1.5
Outputs:
- new_residual: bfloat16 [8192, 3584], P(('dp', 'ep')), parts along dimension 0
- next_q: bfloat16 [8192, 3584], P(('dp', 'ep')), parts along dimension 0
- next_scale: float32 [8192, 28], P(('dp', 'ep')), parts along dimension 0
There are 4 independent parts, one for each index of `dp`. A program takes and returns all parts, laid end to end along the dimension named above; an argument that names none is the same for every part. Nothing has to cross between parts.
Inputs may be any that keep to these rules, and one draw needn't show every extreme that they name: `expert_ids`: each row names 8 different experts; among the rows of one device no expert is named by more than 32 rows, and in some devices one expert is named by exactly 32.
All inputs are finite; a program needn't handle non-finite values.
Results may differ from a plain program's by a relative error of at most 0.015.
Values may be sent and summed in bfloat16 or wider, within the bound.
A program may use at most 192 MiB of HBM per device.

v0:
```python
import jax
import jax.numpy as jnp
from jax import lax
from jax.sharding import PartitionSpec as P


def slot_of(flat_ids, experts):
    hot = (flat_ids[:, None] == jnp.arange(experts, dtype=jnp.int32)[None, :]).astype(jnp.int32)
    before = jnp.cumsum(hot, axis=0) - hot
    return jnp.sum(before * hot, axis=1)


def expert_rows(payload, scales, gates, matrices):
    count = payload.shape[0]
    width = payload.shape[1]
    blocks = (
        payload.astype(jnp.float32).reshape(count, scales.shape[1], width // scales.shape[1])
        * scales[:, :, None]
    )
    inputs = blocks.reshape(count, width).astype(jnp.bfloat16)
    gate_part = jnp.dot(inputs, matrices[0], preferred_element_type=jnp.float32)
    up_part = jnp.dot(inputs, matrices[1], preferred_element_type=jnp.float32)
    hidden = (jax.nn.silu(gate_part) * up_part).astype(jnp.bfloat16)
    output = jnp.dot(hidden, matrices[2], preferred_element_type=jnp.float32)
    return (output * gates[:, None]).astype(jnp.bfloat16)


def per_device(
    tokens_q, token_scale, residual, expert_ids, gate_values, w_gate, w_up, w_down, norm_gain
):
    devices = lax.axis_size("ep")
    local_tokens = tokens_q.shape[0]
    chosen = expert_ids.shape[1]
    width = tokens_q.shape[1]
    blocks_row = token_scale.shape[1]
    capacity = min(local_tokens, 2 * local_tokens * chosen // devices)
    matrices = (w_gate[0], w_up[0], w_down[0])
    assigned = local_tokens * chosen
    owner_local = jnp.arange(assigned, dtype=jnp.int32) // chosen
    flat_ids = expert_ids.reshape(-1)
    target = flat_ids * capacity + slot_of(flat_ids, devices)
    send_payload = (
        jnp.zeros((devices * capacity, width), jnp.bfloat16)
        .at[target]
        .set(tokens_q[owner_local])
        .reshape(devices, capacity, width)
    )
    send_scales = (
        jnp.zeros((devices * capacity, blocks_row), jnp.float32)
        .at[target]
        .set(token_scale[owner_local])
        .reshape(devices, capacity, blocks_row)
    )
    send_gates = (
        jnp.zeros((devices * capacity,), jnp.float32)
        .at[target]
        .set(gate_values.reshape(-1))
        .reshape(devices, capacity)
    )
    part_payload = lax.all_to_all(send_payload, "ep", split_axis=0, concat_axis=0, tiled=True)
    part_scales = lax.all_to_all(
        send_scales.astype(jnp.bfloat16), "ep", split_axis=0, concat_axis=0, tiled=True
    ).astype(send_scales.dtype)
    part_gates = lax.all_to_all(
        send_gates.astype(jnp.bfloat16), "ep", split_axis=0, concat_axis=0, tiled=True
    ).astype(send_gates.dtype)
    rows_count = part_payload.shape[0] * part_payload.shape[1]
    result = expert_rows(
        part_payload.reshape(rows_count, width),
        part_scales.reshape(rows_count, blocks_row),
        part_gates.reshape(rows_count),
        matrices,
    )
    output = result.reshape(part_payload.shape)
    returned = lax.all_to_all(output, "ep", split_axis=0, concat_axis=0, tiled=True).reshape(
        devices * capacity, width
    )
    total = jnp.sum(
        returned[target].reshape(local_tokens, chosen, width).astype(jnp.float32), axis=1
    )
    mixed = total + residual.astype(jnp.float32)
    new_residual = mixed.astype(jnp.bfloat16)
    meansq = jnp.mean(mixed * mixed, axis=-1, keepdims=True)
    normed = mixed * lax.rsqrt(meansq + 1e-06) * norm_gain
    blocks = normed.reshape(local_tokens, blocks_row, width // blocks_row)
    next_scale = (jnp.max(jnp.abs(blocks), axis=-1) + 1e-06) / 448.0
    next_q = (blocks / next_scale[:, :, None]).reshape(local_tokens, width).astype(jnp.bfloat16)
    return (new_residual, next_q, next_scale)


def solution(mesh):
    in_specs = (
        P(("dp", "ep"), None),
        P(("dp", "ep"), None),
        P(("dp", "ep"), None),
        P(("dp", "ep"), None),
        P(("dp", "ep"), None),
        P("ep", None, None),
        P("ep", None, None),
        P("ep", None, None),
        P(),
    )
    out_specs = (P(("dp", "ep"), None), P(("dp", "ep"), None), P(("dp", "ep"), None))
    return jax.shard_map(
        per_device, mesh=mesh, in_specs=in_specs, out_specs=out_specs, check_vma=False
    )
```

profile of v0, /device:TPU:48, one launch (start us, length us, event | category | flops | bytes accessed | tf_op | source)
XLA Modules:
  0.0 375.5 jit_solution(1039579330630566048)
XLA Ops:
  0.6 0.0 copy-start
  0.6 0.8 copy.23
  1.5 0.1 eq.29
  1.6 0.1 eq.25
  1.7 0.7 broadcast_multiply_fusion
  2.4 1.2 reduce-window.6
  3.5 0.2 slice_reduce_fusion
  3.8 0.1 copy.22
  3.9 0.1 mul.80
  4.0 0.8 copy.28
  4.7 0.1 reshape.234
  4.8 0.1 fusion.18
  5.0 2.4 scatter_custom_fusion.2
  7.4 0.7 convert_element_type.115
  8.1 8.0 %all-to-all-start.2 = ((bf16[32,1,32]{2,1,0:T(2,128)(2,1)}), bf16[32,1,32]{2,1,0:T(2,128)(2,1)S(1)}, u32[]{:S(2)}, u32[]{:S(2)}) async-start(bf16[32,1,32]{2,1,0:T(2,128)(2,1)} %convert_element_type.115), calls=%async_computation.2 | async-start | bytes 32768 | tf_op jit(solution)/shard_map/all_to_all | solution.py:64
  16.1 0.8 copy.26
  16.9 3.4 scatter_custom_fusion.1
  20.3 0.9 reshape.260
  21.3 0.0 all-to-all-done.2
  21.3 7.7 %all-to-all-start.1 = ((bf16[32,2,448]{2,1,0:T(2,128)(2,1)}), bf16[32,2,448]{2,1,0:T(2,128)(2,1)S(1)}, u32[]{:S(2)}, u32[]{:S(2)}) async-start(bf16[32,2,448]{2,1,0:T(2,128)(2,1)} %reshape.260), calls=%async_computation.1 | async-start | bytes 131072 | tf_op jit(solution)/shard_map/all_to_all | solution.py:61
  29.0 0.0 copy-done
  29.0 21.1 %scatter_custom_fusion = bf16[1024,3584]{1,0:T(8,128)(2,1)} fusion(s32[512]{0:T(512)S(1)} %bitcast.60, bf16[64,3584]{1,0:T(8,128)(2,1)S(1)} %copy-done, s32[1024]{0:T(1024)S(1)} %pad_clamp_fusion.1, bf16[]{:T(256)} %constant.16.clone.1), kind=kCustom, calls=%fused_computation.15 | custom fusion | bytes 7340034 | tf_op jit(solution)/shard_map/scatter | solution.py:45
  50.0 0.0 all-to-all-done.1
  50.0 7.8 %all-to-all-start = ((bf16[32,32,3584]{2,1,0:T(8,128)(2,1)}), bf16[32,32,3584]{2,1,0:T(8,128)(2,1)}, u32[]{:S(2)}, u32[]{:S(2)}) async-start(bf16[32,32,3584]{2,1,0:T(8,128)(2,1)} %bitcast.52), calls=%async_computation | async-start | bytes 14680064 | tf_op jit(solution)/shard_map/all_to_all | solution.py:60
  57.8 0.1 convert_reduce_fusion.1
  57.9 0.1 reshape.188
  58.0 0.4 reshape.261
  58.3 0.1 bitcast_convert_fusion
  58.4 108.5 %all-to-all-done = bf16[32,32,3584]{2,1,0:T(8,128)(2,1)} async-done(((bf16[32,32,3584]{2,1,0:T(8,128)(2,1)}), bf16[32,32,3584]{2,1,0:T(8,128)(2,1)}, u32[]{:S(2)}, u32[]{:S(2)}) %all-to-all-start) | async-done | bytes 7340064 | tf_op jit(solution)/shard_map/all_to_all | solution.py:60
  166.9 13.6 %reshape.186 = f32[1024,28,128]{2,1,0:T(8,128)} reshape(bf16[32,32,3584]{2,1,0:T(8,128)(2,1)} %all-to-all-done) | data formatting | bytes 22020096 | tf_op jit(solution)/shard_map/convert_element_type | solution.py:17
  180.5 12.7 %multiply_convert_fusion = bf16[1024,28,128]{2,1,0:T(8,128)(2,1)} fusion(f32[1024,28,128]{2,1,0:T(8,128)} %reshape.186, f32[1024,28]{1,0:T(8,128)S(1)} %bitcast_convert_fusion), kind=kLoop, calls=%fused_computation.6 | loop fusion | flops 7340032 | bytes 22134784 | tf_op jit(solution)/shard_map/convert_element_type | solution.py:20
  193.2 12.0 %copy.27 = bf16[1024,28,128]{0,2,1:T(8,128)(2,1)} copy(bf16[1024,28,128]{2,1,0:T(8,128)(2,1)} %multiply_convert_fusion) | data formatting | bytes 14680064 | tf_op jit(solution)/shard_map/convert_element_type | solution.py:20
  205.1 11.8 %fusion.1 = f32[1024,1024]{1,0:T(8,128)S(1)} fusion(bf16[1024,3584]{0,1:T(8,128)(2,1)} %bitcast.54, bf16[1,3584,1024]{2,1,0:T(8,128)(2,1)} %param.15), kind=kOutput, calls=%fused_computation.10 | convolution fusion | flops 7516192768 | bytes 18874368 | tf_op jit(solution)/shard_map/dot_general | solution.py:22
  216.9 0.0 copy-done.2
  216.9 0.0 slice-start.1
  216.9 10.9 %multiply_convert_fusion.2 = bf16[1024,1024]{1,0:T(8,128)(2,1)S(1)} fusion(f32[1024,1024]{1,0:T(8,128)S(1)} %fusion.1, bf16[1024,3584]{0,1:T(8,128)(2,1)S(1)} %bitcast.55, bf16[1,3584,1024]{2,1,0:T(8,128)(2,1)} %param.14), kind=kOutput, calls=%fused_computation.14 | convolution fusion | flops 7522484224 | bytes 20971520 | tf_op jit(solution)/shard_map/dot_general | solution.py:21
  227.8 9.9 %multiply_convert_fusion.1 = bf16[1024,3584]{1,0:T(8,128)(2,1)} fusion(bf16[1024,1024]{1,0:T(8,128)(2,1)S(1)} %multiply_convert_fusion.2, bf16[1,1024,3584]{2,1,0:T(8,128)(2,1)S(1)} %bitcast.65, f32[1024]{0:T(1024)S(1)} %reshape.188), kind=kOutput, calls=%fused_computation.7 | convolution fusion | flops 7523532800 | bytes 16781312 | tf_op jit(solution)/shard_map/dot_general | solution.py:24
  237.7 6.3 %all-to-all-start.3 = ((bf16[32,32,3584]{2,1,0:T(8,128)(2,1)}), bf16[32,32,3584]{2,1,0:T(8,128)(2,1)}, u32[]{:S(2)}, u32[]{:S(2)}) async-start(bf16[32,32,3584]{2,1,0:T(8,128)(2,1)} %bitcast.53), calls=%async_computation.3 | async-start | bytes 14680064 | tf_op jit(solution)/shard_map/all_to_all | solution.py:75
  244.1 109.0 %all-to-all-done.3 = bf16[32,32,3584]{2,1,0:T(8,128)(2,1)} async-done(((bf16[32,32,3584]{2,1,0:T(8,128)(2,1)}), bf16[32,32,3584]{2,1,0:T(8,128)(2,1)}, u32[]{:S(2)}, u32[]{:S(2)}) %all-to-all-start.3) | async-done | bytes 7340064 | tf_op jit(solution)/shard_map/all_to_all | solution.py:75
  353.1 12.0 %gather_fusion = bf16[512,3584]{1,0:T(8,128)(2,1)} fusion(bf16[1024,3584]{1,0:T(8,128)(2,1)} %bitcast.12, s32[1024]{0:T(1024)S(1)} %pad_clamp_fusion), kind=kCustom, calls=%fused_computation.2 | custom fusion | bytes 7342080 | tf_op jit(solution)/shard_map/gather | solution.py:79
  365.1 4.5 %convert_reduce_fusion = f32[64,3584]{1,0:T(8,128)S(1)} fusion(bf16[512,3584]{1,0:T(8,128)(2,1)} %gather_fusion), kind=kLoop, calls=%fused_computation.8 | loop fusion | flops 3440640 | bytes 4587520 | tf_op jit(solution)/shard_map/reduce_sum | solution.py:78
  369.6 0.2 multiply_reduce_fusion
  369.8 1.1 fusion.11
  370.9 1.4 abs.7
  372.3 0.3 reduce_max.9
  372.7 0.7 copy.30
  373.3 0.3 div.44
  373.7 1.6 fusion.10
  (22 shorter events, 0.1 us)
Async XLA Ops:
  0.6 28.3 %copy-start = (bf16[64,3584]{1,0:T(8,128)(2,1)S(1)}, bf16[64,3584]{1,0:T(8,128)(2,1)}, u32[]{:S(2)}) copy-start(bf16[64,3584]{1,0:T(8,128)(2,1)} %param.9) | copy-start | bytes 1376260
  8.1 13.2 %all-to-all-start.2 = ((bf16[32,1,32]{2,1,0:T(2,128)(2,1)}), bf16[32,1,32]{2,1,0:T(2,128)(2,1)S(1)}, u32[]{:S(2)}, u32[]{:S(2)}) async-start(bf16[32,1,32]{2,1,0:T(2,128)(2,1)} %convert_element_type.115), calls=%async_computation.2 | async-start | bytes 32768 | tf_op jit(solution)/shard_map/all_to_all | solution.py:64
  21.3 28.8 %all-to-all-start.1 = ((bf16[32,2,448]{2,1,0:T(2,128)(2,1)}), bf16[32,2,448]{2,1,0:T(2,128)(2,1)S(1)}, u32[]{:S(2)}, u32[]{:S(2)}) async-start(bf16[32,2,448]{2,1,0:T(2,128)(2,1)} %reshape.260), calls=%async_computation.1 | async-start | bytes 131072 | tf_op jit(solution)/shard_map/all_to_all | solution.py:61
  50.0 116.8 %all-to-all-start = ((bf16[32,32,3584]{2,1,0:T(8,128)(2,1)}), bf16[32,32,3584]{2,1,0:T(8,128)(2,1)}, u32[]{:S(2)}, u32[]{:S(2)}) async-start(bf16[32,32,3584]{2,1,0:T(8,128)(2,1)} %bitcast.52), calls=%async_computation | async-start | bytes 14680064 | tf_op jit(solution)/shard_map/all_to_all | solution.py:60
  205.1 11.8 %copy-start.2 = (bf16[1024,28,128]{0,2,1:T(8,128)(2,1)S(1)}, bf16[1024,28,128]{0,2,1:T(8,128)(2,1)}, u32[]{:S(2)}) copy-start(bf16[1024,28,128]{0,2,1:T(8,128)(2,1)} %copy.27) | copy-start | bytes 22020100
  205.1 22.7 %slice-start = ((s8[7340032]{0:T(1024)(128)(4,1)}), s8[4194304]{0:T(1024)(128)(4,1)S(1)}, s32[]{:S(2)}) async-start(s8[7340032]{0:T(1024)(128)(4,1)} %bitcast.64), calls=%async_computation.4 | async-start | bytes 8388608
  216.9 10.9 %slice-start.1 = ((s8[7340032]{0:T(1024)(128)(4,1)}), s8[3145728]{0:T(1024)(128)(4,1)S(1)}, s32[]{:S(2)}) async-start(s8[7340032]{0:T(1024)(128)(4,1)} %bitcast.64), calls=%async_computation.5 | async-start | bytes 6291456
  237.7 115.4 %all-to-all-start.3 = ((bf16[32,32,3584]{2,1,0:T(8,128)(2,1)}), bf16[32,32,3584]{2,1,0:T(8,128)(2,1)}, u32[]{:S(2)}, u32[]{:S(2)}) async-start(bf16[32,32,3584]{2,1,0:T(8,128)(2,1)} %bitcast.53), calls=%async_computation.3 | async-start | bytes 14680064 | tf_op jit(solution)/shard_map/all_to_all | solution.py:75
  353.1 16.5 %copy-start.3 = (bf16[64,3584]{1,0:T(8,128)(2,1)S(1)}, bf16[64,3584]{1,0:T(8,128)(2,1)}, u32[]{:S(2)}) copy-start(bf16[64,3584]{1,0:T(8,128)(2,1)} %param.11) | copy-start | bytes 1376260
  353.1 16.7 %copy-start.4 = (f32[3584]{0:T(1024)S(1)}, f32[3584]{0:T(1024)}, u32[]{:S(2)}) copy-start(f32[3584]{0:T(1024)} %param.17) | copy-start | bytes 43012
  353.1 22.2 %copy-start.1 = (bf16[64,3584]{1,0:T(8,128)(2,1)S(1)}, bf16[64,3584]{1,0:T(8,128)(2,1)}, u32[]{:S(2)}) copy-start(bf16[64,3584]{1,0:T(8,128)(2,1)} %param.9) | copy-start | bytes 1376260
where the time goes:
time: 381 us; the launch traced here: 376 us
  waiting for transfers between devices  218 us (57%)
  local copies, waits for them, and re-layouts  72 us (19%)
  matrix products  32.5 us (9%)
  starting transfers between devices  29.7 us (8%)
  other arithmetic  22.6 us (6%)
    all_to_all x1, waiting for transfers between devices, per_device(): lax.all_to_all(output, 'ep', split_axis=0, concat_axis=0, tiled=True)  109 us
    all_to_all x1, waiting for transfers between devices, per_device(): lax.all_to_all(send_payload, 'ep', split_axis=0, concat_axis=0, tiled=True)  108 us
    scatter x1, local copies, waits for them, and re-layouts, per_device(): send_payload = jnp.zeros((devices * capacity, width), jnp.bfloat16).at[ta...  21.1 us
    convert_element_type x1, local copies, waits for them, and re-layouts, expert_rows(): payload.astype(jnp.float32)  13.6 us
    convert_element_type x1, other arithmetic, expert_rows(): inputs = blocks.reshape(count, width).astype(jnp.bfloat16)  12.7 us
    gather x1, local copies, waits for them, and re-layouts, per_device(): returned[target].reshape(local_tokens, chosen, width).astype(jnp.float32)  12 us
    convert_element_type x1, local copies, waits for them, and re-layouts, expert_rows(): inputs = blocks.reshape(count, width).astype(jnp.bfloat16)  12 us
    dot_general x1, matrix products, expert_rows(): up_part = jnp.dot(inputs, matrices[1], preferred_element_type=jnp.float32)  11.8 us
  transfers between devices with their start and end apart: 4, of which 2 were waited for; matrix products, arithmetic and copies ran while one was open for 7% of the time, Pallas kernels for 0%

commit v1 on v0

v1 whole, which is shorter than its diff:
```python
import functools

import jax
import jax.numpy as jnp
from jax import lax
from jax.experimental import pallas as pl
from jax.experimental.pallas import tpu as pltpu
from jax.sharding import PartitionSpec as P

MESH = pl.DeviceIdType.MESH
F32 = jnp.float32
BF16 = jnp.bfloat16

BATCHES = (
    ((0, 0), (0, 1), (0, 3), (0, 2)),
    ((3, 0), (1, 0), (3, 1), (1, 3)),
    ((3, 3), (1, 1), (3, 2), (1, 2)),
    ((2, 0), (2, 1), (2, 3), (2, 2)),
)
PLACE = {c: (i, j) for i, b in enumerate(BATCHES) for j, c in enumerate(b)}


def dot(a, b):
    return jnp.dot(a, b, preferred_element_type=F32)


def kernel(
    cap,
    tq, ts, res, ids, gv, gain, wg_hbm, wu_hbm, wd_hbm,
    nr_out, nq_out, ns_out,
    XO, WG, WU, WD, S, RF, RN, QF, Q, XS, H, PF, PB, PT, GS, T, TL, MX,
    w_sem, t_send, t_recv, ag_send, ag_recv, dd_send, dd_recv, s_send, s_recv, r1_send, r1_recv, r2_send, r2_recv,
):
    rows, width = tq.shape
    half = rows // 2
    hidden = wg_hbm.shape[1]
    qb = width // ts.shape[1]
    group = 4 * rows
    slots = 4 * cap
    tile = 512 if width % 512 == 0 else 256
    htile = 256

    ep = lax.axis_index("ep")
    core = ep % 2
    z = (ep // 2) % 4
    y = ep // 8

    def device(da, db, other=False):
        yy = (y + da * (1 - core) + db * core) % 4
        zz = (z + da * core + db * (1 - core)) % 4
        cc = (1 - core) if other else core
        return {"ep": (yy * 4 + zz) * 2 + cc}

    plus_a, minus_a = device(1, 0), device(3, 0)
    plus_b, minus_b = device(0, 1), device(0, 3)
    partner = device(0, 0, True)

    barrier = pltpu.get_barrier_semaphore()

    def greet(k, carry):
        pl.semaphore_signal(barrier, inc=1, device_id={"ep": (ep + k) % 32}, device_id_type=MESH)
        return carry

    lax.fori_loop(1, 32, greet, 0)

    loads = [
        pltpu.make_async_copy(src, dst, w_sem.at[n])
        for n, (src, dst) in enumerate(((wg_hbm, WG), (wu_hbm, WU), (wd_hbm, WD)))
    ]
    for c in loads:
        c.start()

    def xin(db, da, stream=0):
        i, j = PLACE[(db, da)]
        return XO.at[stream, i + 1, pl.ds(rows * j, rows), :]

    def xout(db, da):
        i, j = PLACE[(db, da)]
        return XO.at[0, i, pl.ds(rows * j, rows), :]

    lo = rows * PLACE[(0, 0)][1]
    for n in range(width // qb):
        block = tq[:, n * qb:(n + 1) * qb].astype(F32) * ts[:, n:n + 1]
        XO[0, 1, lo:lo + rows, n * qb:(n + 1) * qb] = block.astype(BF16)

    lane = lax.broadcasted_iota(jnp.int32, (rows, 128), 1)
    dense = jnp.zeros((rows, 128), F32)
    for k in range(ids.shape[1]):
        dense = dense + jnp.where(ids[:, k:k + 1] == lane, gv[:, k:k + 1], 0.0)
    turned = jnp.concatenate([dense, jnp.zeros((128 - rows, 128), F32)], axis=0).T[0:32]
    before = (
        lax.broadcasted_iota(jnp.int32, (128, 128), 0) < lax.broadcasted_iota(jnp.int32, (128, 128), 1)
    ).astype(F32).astype(BF16)
    rank = dot((turned > 0.0).astype(F32).astype(BF16), before)
    for e in range(32):
        TL[e, 0:1, :] = turned[e:e + 1, :]
        TL[e, 1:2, :] = rank[e:e + 1, :]
    PF[...] = jnp.zeros_like(PF)

    pl.semaphore_wait(barrier, 31)

    def remote(src, dst, send, recv, who):
        c = pltpu.make_async_remote_copy(
            src_ref=src, dst_ref=dst, send_sem=send, recv_sem=recv, device_id=who, device_id_type=MESH
        )
        return c

    ag = {}

    def gather_move(key, src, dst, who):
        n = len(ag)
        ag[key] = remote(src, dst, ag_send.at[n], ag_recv.at[n], who)

    top, low = pl.ds(0, half), pl.ds(half, half)
    gather_move(("a", 3), xin(0, 0), xin(0, 3), plus_a)
    gather_move(("a", 1), xin(0, 0), xin(0, 1), minus_a)
    gather_move(("a", "2t"), xin(0, 3).at[top, :], xin(0, 2).at[top, :], plus_a)
    gather_move(("a", "2l"), xin(0, 1).at[low, :], xin(0, 2).at[low, :], minus_a)
    for da in range(4):
        gather_move((3, da), xin(0, da), xin(3, da), plus_b)
        gather_move((1, da), xin(0, da), xin(1, da), minus_b)
    for da in (0, 1):
        gather_move((2, da), xin(3, da), xin(2, da), plus_b)
    for da in (3, 2):
        gather_move((2, da), xin(1, da), xin(2, da), minus_b)
    dd = {}
    for c, (i, j) in PLACE.items():
        n = 4 * i + j
        dd[c] = remote(xin(*c), xin(*c, stream=1), dd_send.at[n], dd_recv.at[n], partner)

    ag[("a", 3)].start()
    ag[("a", 1)].start()
    ag[(3, 0)].start()
    ag[(1, 0)].start()
    dd[(0, 0)].start()

    tables = []
    for s in range(2):
        for (db, da), (i, j) in PLACE.items():
            n = 16 * s + 4 * i + j
            if n == 0:
                continue
            who = device(4 - da, 4 - db, s == 1)
            c = remote(TL.at[who["ep"]], T.at[n], t_send.at[n], t_recv.at[n], who)
            c.start()
            tables.append(c)
    T[0] = TL[ep]

    ag[("a", 3)].wait_recv()
    ag[("a", "2t")].start()
    ag[(3, 3)].start()
    ag[(1, 3)].start()
    dd[(0, 3)].start()
    ag[("a", 1)].wait_recv()
    ag[("a", "2l")].start()
    ag[(3, 1)].start()
    ag[(1, 1)].start()
    dd[(0, 1)].start()
    ag[("a", "2t")].wait_recv()
    ag[("a", "2l")].wait_recv()
    ag[(3, 2)].start()
    ag[(1, 2)].start()
    dd[(0, 2)].start()
    for c in tables:
        c.wait_recv()

    def arrived(db, da):
        ag[(db, da)].wait_recv()
        dd[(db, da)].start()
        if (db == 3 and da in (0, 1)) or (db == 1 and da in (3, 2)):
            ag[(2, da)].start()

    arrived(3, 0)
    arrived(1, 0)

    def tables_of(i):
        slot = lax.broadcasted_iota(jnp.int32, (cap, 128), 0).astype(F32)
        for s in range(2):
            for j in range(4):
                t = T[16 * s + 4 * i + j]
                gate, place = t[0:1, :], t[1:2, :]
                pick = jnp.where((slot == place) & (gate > 0.0), 1.0, 0.0)
                weight = jnp.sum(pick * gate, axis=1, keepdims=True)
                GS[slots * s + cap * j:slots * s + cap * (j + 1), :] = jnp.broadcast_to(weight, (cap, 128))
                if rows == 64 and j % 2 == 1:
                    pick = pltpu.roll(pick, 64, 1)
                block = 128 * (rows * j // 128)
                PF[s, cap * j:cap * (j + 1), block:block + 128] = pick
            PB[s] = PF[s].astype(BF16)
            PT[s] = PF[s].T.astype(BF16)

    def gather_rows(i, s):
        def step(n, carry):
            cols = pl.ds(pl.multiple_of(n * tile, tile), tile)
            XS[slots * s:slots * (s + 1), cols] = dot(PB[s], XO[s, i + 1, :, cols]).astype(BF16)
            return carry

        lax.fori_loop(0, width // tile, step, 0)

    def gate_up():
        def step(n, carry):
            cols = pl.ds(pl.multiple_of(n * htile, htile), htile)
            g = dot(XS[...], WG[:, cols])
            u = dot(XS[...], WU[:, cols])
            H[:, cols] = (g / (1.0 + jnp.exp(-g)) * u).astype(BF16)
            return carry

        lax.fori_loop(0, hidden // htile, step, 0)

    def down(i):
        def step(n, carry):
            cols = pl.ds(pl.multiple_of(n * tile, tile), tile)
            part = (dot(H[...], WD[:, cols]) * GS[:, 0:1]).astype(BF16)
            for s in range(2):
                XO[s, i, :, cols] = dot(PT[s], part[slots * s:slots * (s + 1)]).astype(BF16)
            return carry

        lax.fori_loop(0, width // tile, step, 0)

    step_rows = 16

    def add_into(dst, src):
        def step(n, carry):
            r = pl.ds(pl.multiple_of(n * step_rows, step_rows), step_rows)
            dst[r, :] = (dst[r, :].astype(F32) + src[r, :].astype(F32)).astype(BF16)
            return carry

        lax.fori_loop(0, dst.shape[0] // step_rows, step, 0)

    swap = [
        remote(XO.at[1, i], S.at[i], s_send.at[i], s_recv.at[i], partner) for i in range(4)
    ]

    def merge(i):
        swap[i].wait_recv()
        add_into(XO.at[0, i], S.at[i])

    r1 = {}

    def r1_move(key, src, dst, who):
        n = len(r1)
        r1[key] = remote(src, dst, r1_send.at[n], r1_recv.at[n], who)

    for n, da in enumerate((1, 0)):
        r1_move(("f", 0, n), xout(2, da), RF.at[0, n], plus_b)
    for n, da in enumerate((2, 3)):
        r1_move(("f", 1, n), xout(2, da), RF.at[1, n], minus_b)
    for da in range(4):
        r1_move(("n", 0, da), xout(1, da), RN.at[0, da], plus_b)
        r1_move(("n", 1, da), xout(3, da), RN.at[1, da], minus_b)

    def sent(i):
        for (db, da) in BATCHES[i]:
            dd[(db, da)].wait_send()
        if i == 0:
            for key in (("a", 3), ("a", 1), ("a", "2t"), ("a", "2l")):
                ag[key].wait_send()
            for da in range(4):
                ag[(3, da)].wait_send()
                ag[(1, da)].wait_send()
        for (db, da) in BATCHES[i]:
            if (db == 3 and da in (0, 1)) or (db == 1 and da in (3, 2)):
                ag[(2, da)].wait_send()

    for c in loads[:2]:
        c.wait()

    for i in range(4):
        tables_of(i)
        gather_rows(i, 0)
        for c in BATCHES[i]:
            dd[c].wait_recv()
        gather_rows(i, 1)
        gate_up()
        if i == 0:
            loads[2].wait()
            arrived(3, 1)
            arrived(1, 3)
        elif i == 1:
            arrived(3, 3)
            arrived(1, 1)
            merge(0)
        elif i == 2:
            merge(1)
            r1[("n", 0, 3)].start()
            r1[("n", 1, 1)].start()
            r1[("n", 1, 0)].start()
            arrived(2, 0)
            arrived(2, 3)
        elif i == 3:
            merge(2)
            r1[("n", 0, 2)].start()
        if i > 0:
            sent(i - 1)
        down(i)
        swap[i].start()
        if i == 1:
            arrived(3, 2)
            arrived(1, 2)
        elif i == 2:
            arrived(2, 1)
            arrived(2, 2)
    merge(3)
    for key in (("f", 0, 0), ("f", 1, 0), ("f", 0, 1), ("f", 1, 1)):
        r1[key].start()

    for n in range(2):
        da = (1, 0)[n]
        r1[("f", 0, n)].wait_recv()
        add_into(xout(1, da), RF.at[0, n])
        r1[("n", 0, da)].start()
        da = (2, 3)[n]
        r1[("f", 1, n)].wait_recv()
        add_into(xout(3, da), RF.at[1, n])
        r1[("n", 1, da)].start()

    def collect(da):
        r1[("n", 0, da)].wait_recv()
        r1[("n", 1, da)].wait_recv()
        dst, p, m = xout(0, da), RN.at[0, da], RN.at[1, da]

        def step(n, carry):
            r = pl.ds(pl.multiple_of(n * step_rows, step_rows), step_rows)
            dst[r, :] = (dst[r, :].astype(F32) + p[r, :].astype(F32) + m[r, :].astype(F32)).astype(BF16)
            return carry

        lax.fori_loop(0, rows // step_rows, step, 0)

    r2 = [
        remote(xout(0, 2).at[top, :], QF.at[0], r2_send.at[0], r2_recv.at[0], plus_a),
        remote(xout(0, 2).at[low, :], QF.at[1], r2_send.at[1], r2_recv.at[1], minus_a),
        remote(xout(0, 1).at[low, :], Q.at[0].at[low, :], r2_send.at[2], r2_recv.at[2], plus_a),
        remote(xout(0, 3).at[top, :], Q.at[1].at[top, :], r2_send.at[3], r2_recv.at[3], minus_a),
        remote(xout(0, 1).at[top, :], Q.at[0].at[top, :], r2_send.at[4], r2_recv.at[4], plus_a),
        remote(xout(0, 3).at[low, :], Q.at[1].at[low, :], r2_send.at[5], r2_recv.at[5], minus_a),
    ]
    collect(2)
    r2[0].start()
    r2[1].start()
    collect(1)
    r2[2].start()
    collect(3)
    r2[3].start()
    r2[0].wait_recv()
    add_into(xout(0, 1).at[top, :], QF.at[0])
    r2[4].start()
    r2[1].wait_recv()
    add_into(xout(0, 3).at[low, :], QF.at[1])
    r2[5].start()

    r1[("n", 0, 0)].wait_recv()
    r1[("n", 1, 0)].wait_recv()
    mine = xout(0, 0)

    def start_sum(n, carry):
        r = pl.ds(pl.multiple_of(n * step_rows, step_rows), step_rows)
        MX[r, :] = (
            res[r, :].astype(F32)
            + mine[r, :].astype(F32)
            + RN[0, 0, r, :].astype(F32)
            + RN[1, 0, r, :].astype(F32)
        )
        return carry

    lax.fori_loop(0, rows // step_rows, start_sum, 0)
    for n in (2, 3, 4, 5):
        r2[n].wait_recv()

    def finish(n, carry):
        r = pl.ds(pl.multiple_of(n * step_rows, step_rows), step_rows)
        mixed = MX[r, :] + Q[0, r, :].astype(F32) + Q[1, r, :].astype(F32)
        nr_out[r, :] = mixed.astype(BF16)
        meansq = jnp.mean(mixed * mixed, axis=-1, keepdims=True)
        normed = mixed * lax.rsqrt(meansq + 1e-06) * gain[...]
        lanes = lax.broadcasted_iota(jnp.int32, (step_rows, 128), 1)
        scales = jnp.zeros((step_rows, 128), F32)
        for b in range(width // qb):
            block = normed[:, b * qb:(b + 1) * qb]
            scale = (jnp.max(jnp.abs(block), axis=-1, keepdims=True) + 1e-06) / 448.0
            nq_out[r, b * qb:(b + 1) * qb] = (block / scale).astype(BF16)
            scales = jnp.where(lanes == b, scale, scales)
        ns_out[r, :] = scales[:, 0:width // qb]
        return carry

    lax.fori_loop(0, rows // step_rows, finish, 0)

    for i in (3,):
        sent(i)
    for c in swap:
        c.wait_send()
    for c in tables:
        c.wait_send()
    for c in r1.values():
        c.wait_send()
    for c in r2:
        c.wait_send()


def per_device(
    tokens_q, token_scale, residual, expert_ids, gate_values, w_gate, w_up, w_down, norm_gain
):
    rows, width = tokens_q.shape
    hidden = w_gate.shape[2]
    cap = rows // 2
    vmem = pl.BlockSpec(memory_space=pltpu.VMEM)
    hbm = pl.BlockSpec(memory_space=pl.ANY)
    dma = pltpu.SemaphoreType.DMA
    return pl.pallas_call(
        functools.partial(kernel, cap),
        out_shape=(
            jax.ShapeDtypeStruct((rows, width), BF16),
            jax.ShapeDtypeStruct((rows, width), BF16),
            jax.ShapeDtypeStruct(token_scale.shape, F32),
        ),
        in_specs=[vmem] * 6 + [hbm] * 3,
        out_specs=(vmem, vmem, vmem),
        scratch_shapes=[
            pltpu.VMEM((2, 5, 4 * rows, width), BF16),
            pltpu.VMEM((width, hidden), BF16),
            pltpu.VMEM((width, hidden), BF16),
            pltpu.VMEM((hidden, width), BF16),
            pltpu.VMEM((4, 4 * rows, width), BF16),
            pltpu.VMEM((2, 2, rows, width), BF16),
            pltpu.VMEM((2, 4, rows, width), BF16),
            pltpu.VMEM((2, rows // 2, width), BF16),
            pltpu.VMEM((2, rows, width), BF16),
            pltpu.VMEM((8 * cap, width), BF16),
            pltpu.VMEM((8 * cap, hidden), BF16),
            pltpu.VMEM((2, 4 * cap, 4 * rows), F32),
            pltpu.VMEM((2, 4 * cap, 4 * rows), BF16),
            pltpu.VMEM((2, 4 * rows, 4 * cap), BF16),
            pltpu.VMEM((8 * cap, 128), F32),
            pltpu.VMEM((32, 2, 128), F32),
            pltpu.VMEM((32, 2, 128), F32),
            pltpu.VMEM((rows, width), F32),
            dma((3,)), dma((32,)), dma((32,)), dma((16,)), dma((16,)), dma((16,)), dma((16,)),
            dma((4,)), dma((4,)), dma((12,)), dma((12,)), dma((6,)), dma((6,)),
        ],
        compiler_params=pltpu.CompilerParams(
            collective_id=0, has_side_effects=True, vmem_limit_bytes=67043328
        ),
    )(
        tokens_q, token_scale, residual, expert_ids, gate_values, norm_gain.reshape(1, width),
        w_gate[0], w_up[0], w_down[0],
    )


def solution(mesh):
    rows = P(("dp", "ep"), None)
    weight = P("ep", None, None)
    return jax.shard_map(
        per_device,
        mesh=mesh,
        in_specs=(rows, rows, rows, rows, rows, weight, weight, weight, P()),
        out_specs=(rows, rows, rows),
        check_vma=False,
    )
```

time: 381 us -> 137 us (0.36)
  the two profiles are of different devices: /device:TPU:48 before, /device:TPU:0 now
where the time goes in v1:
time: 137 us; the launch traced here: 136 us
  Pallas kernels  125 us (91%)
  local copies, waits for them, and re-layouts  10.6 us (8%)
    pallas_call x1, Pallas kernels, per_device(): pl.pallas_call(functools.partial(kernel, cap), out_shape=(jax.ShapeDtypeS...  125 us
    unnamed x5, local copies, waits for them, and re-layouts  7.81 us

profile of v1, /device:TPU:0, one launch (start us, length us, event | category | flops | bytes accessed | tf_op | source)
XLA Modules:
  0.0 136.3 jit_solution(13348264610717962671)
XLA Ops:
  0.6 1.3 reshape.9.gain
  2.0 1.4 %copy.12.ts = f32[64,28]{1,0:T(8,128)} copy(f32[64,28]{0,1:T(8,128)} %param.10) | data formatting | bytes 14336 | tf_op args[1]
  3.4 1.4 %copy.13.ids = s32[64,8]{1,0:T(8,128)} copy(s32[64,8]{0,1:T(8,128)} %param.12) | data formatting | bytes 4096 | tf_op args[3]
  4.8 1.4 %copy.14.gv = f32[64,8]{1,0:T(8,128)} copy(f32[64,8]{0,1:T(8,128)} %param.13) | data formatting | bytes 4096 | tf_op args[4]
  6.1 125.1 %shard_map.112 = (bf16[64,3584]{1,0:T(8,128)(2,1)}, bf16[64,3584]{1,0:T(8,128)(2,1)}, f32[64,28]{1,0:T(8,128)}) custom-call(bf16[64,3584]{1,0:T(8,128)(2,1)} %tq.1, f32[64,28]{1,0:T(8,128)} %copy.12.ts, bf16[64,3584]{1,0:T(8,128)(2,1)} %res.1, s32[64,8]{1,0:T(8,128)} %copy.13.ids, f32[64,8]{1,0:T(8,128)} %copy.14.gv, f32[1,3584]{1,0:T(1,128)} %reshape.9.gain, ...), custom_call_target="tpu_custom_call" | custom-call | tf_op jit(solution)/shard_map/pallas_call | solution.py:408
  131.2 1.4 %copy.15 = f32[64,28]{0,1:T(8,128)} copy(f32[64,28]{1,0:T(8,128)} %get-tuple-element.5) | data formatting | bytes 14336 | tf_op jit(solution)/shard_map/pallas_call | solution.py:408
  132.7 1.8 %copy.18 = bf16[64,3584]{1,0:T(8,128)(2,1)} copy(bf16[64,3584]{1,0:T(8,128)(2,1)} %get-tuple-element.9) | data formatting | bytes 917504
  134.5 1.8 %copy.19 = bf16[64,3584]{1,0:T(8,128)(2,1)} copy(bf16[64,3584]{1,0:T(8,128)(2,1)} %get-tuple-element.10) | data formatting | bytes 917504

commit v2 on v1

v2 whole, which is shorter than its diff:
```python
import functools

import jax
import jax.numpy as jnp
from jax import lax
from jax.experimental import pallas as pl
from jax.experimental.pallas import tpu as pltpu
from jax.sharding import PartitionSpec as P

MESH = pl.DeviceIdType.MESH
F32 = jnp.float32
BF16 = jnp.bfloat16

BATCHES = (
    ((0, 0), (0, 1), (0, 3), (0, 2)),
    ((1, 0), (3, 1), (1, 3), (2, 0)),
    ((2, 2), (2, 3), (2, 1), (3, 0)),
    ((3, 2), (1, 1), (1, 2), (3, 3)),
)
HOLD = (0, 1, 3, 4)
PLACE = {c: (i, j) for i, b in enumerate(BATCHES) for j, c in enumerate(b)}


def tile_of(width):
    return 896 if width % 896 == 0 else 256


def dot(a, b):
    return jnp.dot(a, b, preferred_element_type=F32)


def kernel(
    cap,
    tq, ts, res, ids, gv, wg_hbm, wu_hbm, wd_hbm,
    mixed_out,
    XO, WG, WU, WD, S, RF, RN, QF, Q, H, GU, PV, PF, PB, PT, GS, T, TL, SQ,
    w_sem, t_send, t_recv, ag_send, ag_recv, dd_send, dd_recv, s_send, s_recv, r1_send, r1_recv, r2_send, r2_recv,
):
    rows, width = tq.shape
    half = rows // 2
    hidden = wg_hbm.shape[1]
    qb = width // ts.shape[0]
    group = 4 * rows
    slots = 4 * cap
    tile = tile_of(width)
    htile = 256

    ep = lax.axis_index("ep")
    core = ep % 2
    z = (ep // 2) % 4
    y = ep // 8

    def device(da, db, other=False):
        yy = (y + da * (1 - core) + db * core) % 4
        zz = (z + da * core + db * (1 - core)) % 4
        cc = (1 - core) if other else core
        return {"ep": (yy * 4 + zz) * 2 + cc}

    plus_a, minus_a = device(1, 0), device(3, 0)
    plus_b, minus_b = device(0, 1), device(0, 3)
    partner = device(0, 0, True)

    barrier = pltpu.get_barrier_semaphore()

    def greet(k, carry):
        pl.semaphore_signal(barrier, inc=1, device_id={"ep": (ep + k) % 32}, device_id_type=MESH)
        return carry

    lax.fori_loop(1, 32, greet, 0)

    loads = [
        pltpu.make_async_copy(src, dst, w_sem.at[n])
        for n, (src, dst) in enumerate(((wg_hbm, WG), (wu_hbm, WU), (wd_hbm, WD)))
    ]
    for c in loads:
        c.start()

    def xin(db, da, stream=0):
        i, j = PLACE[(db, da)]
        return XO.at[stream, i + 2, pl.ds(rows * j, rows), :]

    def xout(db, da):
        i, j = PLACE[(db, da)]
        return XO.at[0, i, pl.ds(rows * j, rows), :]

    lo = rows * PLACE[(0, 0)][1]
    SQ[...] = jnp.zeros_like(SQ)
    SQ[0:width // qb, 0:rows] = ts[...]
    scales = SQ[...].T[0:rows]
    for n in range(width // qb):
        block = tq[:, n * qb:(n + 1) * qb].astype(F32) * scales[:, n:n + 1]
        XO[0, 2, lo:lo + rows, n * qb:(n + 1) * qb] = block.astype(BF16)

    expert = lax.broadcasted_iota(jnp.int32, (32, rows), 0)
    gates = jnp.zeros((32, rows), F32)
    for k in range(ids.shape[0]):
        gates = gates + jnp.where(ids[k:k + 1, :] == expert, gv[k:k + 1, :], 0.0)
    before = (
        lax.broadcasted_iota(jnp.int32, (rows, rows), 0) < lax.broadcasted_iota(jnp.int32, (rows, rows), 1)
    ).astype(F32).astype(BF16)
    rank = dot((gates > 0.0).astype(F32).astype(BF16), before)
    TL[...] = jnp.zeros_like(TL)
    for e in range(32):
        TL[e, 0:1, 0:rows] = gates[e:e + 1, :]
        TL[e, 1:2, 0:rows] = rank[e:e + 1, :]
    PF[...] = jnp.zeros_like(PF)

    pl.semaphore_wait(barrier, 31)

    def remote(src, dst, send, recv, who):
        c = pltpu.make_async_remote_copy(
            src_ref=src, dst_ref=dst, send_sem=send, recv_sem=recv, device_id=who, device_id_type=MESH
        )
        return c

    ag = {}
    leaving = {i: [] for i in range(4)}

    def gather_move(key, src_place, src, dst, who):
        n = len(ag)
        ag[key] = remote(src, dst, ag_send.at[n], ag_recv.at[n], who)
        leaving[PLACE[src_place][0]].append(ag[key])

    top, low = pl.ds(0, half), pl.ds(half, half)
    for name, part in (("t", top), ("l", low)):
        gather_move(("a", "3" + name), (0, 0), xin(0, 0).at[part, :], xin(0, 3).at[part, :], plus_a)
        gather_move(("a", "1" + name), (0, 0), xin(0, 0).at[part, :], xin(0, 1).at[part, :], minus_a)
    gather_move(("a", "2t"), (0, 3), xin(0, 3).at[top, :], xin(0, 2).at[top, :], plus_a)
    gather_move(("a", "2l"), (0, 1), xin(0, 1).at[low, :], xin(0, 2).at[low, :], minus_a)
    for da in range(4):
        gather_move((3, da), (0, da), xin(0, da), xin(3, da), plus_b)
        gather_move((1, da), (0, da), xin(0, da), xin(1, da), minus_b)
    for da in (0, 1):
        gather_move((2, da), (3, da), xin(3, da), xin(2, da), plus_b)
    for da in (3, 2):
        gather_move((2, da), (1, da), xin(1, da), xin(2, da), minus_b)
    dd = {}
    for c, (i, j) in PLACE.items():
        n = 4 * i + j
        dd[c] = remote(xin(*c), xin(*c, stream=1), dd_send.at[n], dd_recv.at[n], partner)
        leaving[i].append(dd[c])

    ag[("a", "3t")].start()
    ag[("a", "1l")].start()
    ag[("a", "3l")].start()
    ag[("a", "1t")].start()
    dd[(0, 0)].start()

    tables = []
    for s in range(2):
        for (db, da), (i, j) in PLACE.items():
            n = 16 * s + 4 * i + j
            if n == 0:
                continue
            who = device(4 - da, 4 - db, s == 1)
            c = remote(TL.at[who["ep"]], T.at[n], t_send.at[n], t_recv.at[n], who)
            c.start()
            tables.append(c)
    T[0] = TL[ep]

    def arrived(db, da):
        ag[(db, da)].wait_recv()
        if (db == 3 and da in (0, 1)) or (db == 1 and da in (3, 2)):
            ag[(2, da)].start()
        dd[(db, da)].start()

    def tables_of(i):
        slot = lax.broadcasted_iota(jnp.int32, (cap, 128), 0).astype(F32)
        for s in range(2):
            for j in range(4):
                t = T[16 * s + 4 * i + j]
                gate, place = t[0:1, :], t[1:2, :]
                pick = jnp.where((slot == place) & (gate > 0.0), 1.0, 0.0)
                weight = jnp.sum(pick * gate, axis=1, keepdims=True)
                GS[i, slots * s + cap * j:slots * s + cap * (j + 1), :] = jnp.broadcast_to(weight, (cap, 128))
                if rows == 64 and j % 2 == 1:
                    pick = pltpu.roll(pick, 64, 1)
                block = 128 * (rows * j // 128)
                PF[s, cap * j:cap * (j + 1), block:block + 128] = pick
            PB[i, s] = PF[s].astype(BF16)
            PT[i, s] = PF[s].T.astype(BF16)

    ag[("a", "3t")].wait_recv()
    ag[("a", "2t")].start()
    ag[("a", "1l")].wait_recv()
    ag[("a", "2l")].start()
    ag[(3, 0)].start()
    ag[(1, 0)].start()
    for c in tables:
        c.wait_recv()
    for i in range(2):
        tables_of(i)
    ag[("a", "1t")].wait_recv()
    ag[(3, 1)].start()
    ag[("a", "3l")].wait_recv()
    ag[(1, 3)].start()
    dd[(0, 1)].start()
    dd[(0, 3)].start()
    ag[("a", "2t")].wait_recv()
    ag[("a", "2l")].wait_recv()
    ag[(1, 2)].start()
    dd[(0, 2)].start()
    for i in range(2, 4):
        tables_of(i)
    arrived(3, 0)
    arrived(1, 0)
    ag[(3, 3)].start()

    wide = width // 2 if width % 256 == 0 else width

    def gather_rows(i, s):
        for n in range(width // wide):
            cols = slice(n * wide, (n + 1) * wide)
            XO[0, HOLD[i], slots * s:slots * (s + 1), cols] = dot(PB[i, s], XO[s, i + 2, :, cols]).astype(BF16)

    def gate_up(i):
        def products(n):
            cols = pl.ds(pl.multiple_of(n * htile, htile), htile)
            GU[n % 2, 0] = dot(XO[0, HOLD[i]], WG[:, cols])
            GU[n % 2, 1] = dot(XO[0, HOLD[i]], WU[:, cols])

        def activate(n):
            cols = pl.ds(pl.multiple_of(n * htile, htile), htile)
            g = GU[n % 2, 0]
            H[:, cols] = (g / (1.0 + jnp.exp(-g)) * GU[n % 2, 1]).astype(BF16)

        def step(n, carry):
            activate(n - 1)
            products(n)
            return carry

        products(0)
        lax.fori_loop(1, hidden // htile, step, 0)
        activate(hidden // htile - 1)

    def down(i):
        def part(n):
            cols = pl.ds(pl.multiple_of(n * tile, tile), tile)
            PV[n % 2] = (dot(H[...], WD[:, cols]) * GS[i, :, 0:1]).astype(BF16)

        def spread(n):
            cols = pl.ds(pl.multiple_of(n * tile, tile), tile)
            for s in range(2):
                XO[s, i, :, cols] = dot(PT[i, s], PV[n % 2, slots * s:slots * (s + 1)]).astype(BF16)

        def step(n, carry):
            spread(n - 1)
            part(n)
            return carry

        part(0)
        lax.fori_loop(1, width // tile, step, 0)
        spread(width // tile - 1)

    step_rows = 16

    def add_into(dst, *sources):
        def step(n, carry):
            r = pl.ds(pl.multiple_of(n * step_rows, step_rows), step_rows)
            total = dst[r, :].astype(F32)
            for src in sources:
                total = total + src[r, :].astype(F32)
            dst[r, :] = total.astype(BF16)
            return carry

        lax.fori_loop(0, dst.shape[0] // step_rows, step, 0)

    def part_of(db, da):
        i, j = PLACE[(db, da)]
        return S.at[i, pl.ds(rows * j, rows), :]

    swap = {}
    for c, (i, j) in PLACE.items():
        n = 4 * i + j
        src = XO.at[1, i, pl.ds(rows * j, rows), :]
        swap[c] = remote(src, part_of(*c), s_send.at[n], s_recv.at[n], partner)

    def merge(db, da, *more):
        swap[(db, da)].wait_recv()
        add_into(xout(db, da), part_of(db, da), *more)

    r1 = {}

    def r1_move(key, src, dst, who):
        n = len(r1)
        r1[key] = remote(src, dst, r1_send.at[n], r1_recv.at[n], who)

    far = ((2, 1), (0, 3))
    for n in range(2):
        r1_move(("f", 0, n), xout(2, far[0][n]), RF.at[0, n], plus_b)
        r1_move(("f", 1, n), xout(2, far[1][n]), RF.at[1, n], minus_b)
    for da in range(4):
        r1_move(("n", 0, da), xout(1, da), RN.at[0, da], plus_b)
        r1_move(("n", 1, da), xout(3, da), RN.at[1, da], minus_b)

    def sent(i):
        for c in leaving[i]:
            c.wait_send()

    def pass_on(sign, n):
        db, da = (1, 3)[sign], far[sign][n]
        r1[("f", sign, n)].wait_recv()
        merge(db, da, RF.at[sign, n])
        r1[("n", sign, da)].start()

    def send_far(sign, n):
        merge(2, far[sign][n])
        r1[("f", sign, n)].start()

    def send_near(sign, da):
        merge((1, 3)[sign], da)
        r1[("n", sign, da)].start()

    for c in loads[:2]:
        c.wait()

    for i in range(4):
        for c in BATCHES[i]:
            dd[c].wait_recv()
        if i > 1:
            sent(i - 1)
        gather_rows(i, 0)
        gather_rows(i, 1)
        gate_up(i)
        if i == 0:
            loads[2].wait()
            arrived(3, 1)
            arrived(1, 3)
            ag[(3, 2)].start()
        elif i == 1:
            arrived(3, 3)
            arrived(2, 3)
        elif i == 2:
            send_near(0, 0)
            send_near(1, 1)
            send_near(0, 3)
            send_far(1, 0)
            arrived(3, 2)
            arrived(1, 1)
        elif i == 3:
            send_far(0, 0)
            send_far(1, 1)
            send_far(0, 1)
            pass_on(1, 0)
        if i == 2:
            sent(0)
        down(i)
        for c in BATCHES[i]:
            swap[c].start()
        if i == 0:
            arrived(1, 2)
            ag[(1, 1)].start()
            arrived(2, 0)
        elif i == 1:
            arrived(2, 1)
            arrived(2, 2)
    send_near(1, 2)
    pass_on(0, 0)
    pass_on(1, 1)
    pass_on(0, 1)

    def collect(da):
        r1[("n", 0, da)].wait_recv()
        r1[("n", 1, da)].wait_recv()
        merge(0, da, RN.at[0, da], RN.at[1, da])

    r2 = [
        remote(xout(0, 2).at[top, :], QF.at[0], r2_send.at[0], r2_recv.at[0], plus_a),
        remote(xout(0, 2).at[low, :], QF.at[1], r2_send.at[1], r2_recv.at[1], minus_a),
        remote(xout(0, 1).at[low, :], Q.at[0].at[low, :], r2_send.at[2], r2_recv.at[2], plus_a),
        remote(xout(0, 3).at[top, :], Q.at[1].at[top, :], r2_send.at[3], r2_recv.at[3], minus_a),
        remote(xout(0, 1).at[top, :], Q.at[0].at[top, :], r2_send.at[4], r2_recv.at[4], plus_a),
        remote(xout(0, 3).at[low, :], Q.at[1].at[low, :], r2_send.at[5], r2_recv.at[5], minus_a),
    ]
    collect(2)
    r2[0].start()
    r2[1].start()
    collect(1)
    r2[2].start()
    collect(3)
    r2[3].start()
    r2[0].wait_recv()
    add_into(xout(0, 1).at[top, :], QF.at[0])
    r2[4].start()
    r2[1].wait_recv()
    add_into(xout(0, 3).at[low, :], QF.at[1])
    r2[5].start()

    r1[("n", 0, 0)].wait_recv()
    r1[("n", 1, 0)].wait_recv()
    mine, partners = xout(0, 0), part_of(0, 0)
    swap[(0, 0)].wait_recv()

    def start_sum(n, carry):
        r = pl.ds(pl.multiple_of(n * step_rows, step_rows), step_rows)
        mixed_out[r, :] = (
            res[r, :].astype(F32)
            + mine[r, :].astype(F32)
            + partners[r, :].astype(F32)
            + RN[0, 0, r, :].astype(F32)
            + RN[1, 0, r, :].astype(F32)
        )
        return carry

    lax.fori_loop(0, rows // step_rows, start_sum, 0)
    for n in (2, 3, 4, 5):
        r2[n].wait_recv()

    def finish(n, carry):
        r = pl.ds(pl.multiple_of(n * step_rows, step_rows), step_rows)
        mixed_out[r, :] = mixed_out[r, :] + Q[0, r, :].astype(F32) + Q[1, r, :].astype(F32)
        return carry

    lax.fori_loop(0, rows // step_rows, finish, 0)

    sent(3)
    for c in swap.values():
        c.wait_send()
    for c in tables:
        c.wait_send()
    for c in r1.values():
        c.wait_send()
    for c in r2:
        c.wait_send()


def norm_kernel(mixed_ref, gain, nr_out, nq_out, ns_out, SQ):
    rows, width = mixed_ref.shape
    qb = width // ns_out.shape[0]
    step_rows = 16
    SQ[...] = jnp.zeros_like(SQ)

    def step(n, carry):
        r = pl.ds(pl.multiple_of(n * step_rows, step_rows), step_rows)
        mixed = mixed_ref[r, :]
        nr_out[r, :] = mixed.astype(BF16)
        scaled = lax.rsqrt(jnp.mean(mixed * mixed, axis=-1, keepdims=True) + 1e-06)
        lanes = lax.broadcasted_iota(jnp.int32, (step_rows, 128), 1)
        scales = jnp.zeros((step_rows, 128), F32)
        for b in range(width // qb):
            block = mixed[:, b * qb:(b + 1) * qb] * scaled * gain[b:b + 1, :]
            scale = (jnp.max(jnp.abs(block), axis=-1, keepdims=True) + 1e-06) / 448.0
            nq_out[r, b * qb:(b + 1) * qb] = (block / scale).astype(BF16)
            scales = jnp.where(lanes == b, scale, scales)
        SQ[r, :] = scales
        return carry

    lax.fori_loop(0, rows // step_rows, step, 0)
    ns_out[...] = SQ[...].T[0:width // qb, 0:rows]


def per_device(
    tokens_q, token_scale, residual, expert_ids, gate_values, w_gate, w_up, w_down, norm_gain
):
    rows, width = tokens_q.shape
    blocks = token_scale.shape[1]
    hidden = w_gate.shape[2]
    cap = rows // 2
    vmem = pl.BlockSpec(memory_space=pltpu.VMEM)
    hbm = pl.BlockSpec(memory_space=pl.ANY)
    dma = pltpu.SemaphoreType.DMA
    mixed = pl.pallas_call(
        functools.partial(kernel, cap),
        out_shape=jax.ShapeDtypeStruct((rows, width), F32),
        in_specs=[vmem] * 5 + [hbm] * 3,
        out_specs=vmem,
        scratch_shapes=[
            pltpu.VMEM((2, 6, 4 * rows, width), BF16),
            pltpu.VMEM((width, hidden), BF16),
            pltpu.VMEM((width, hidden), BF16),
            pltpu.VMEM((hidden, width), BF16),
            pltpu.VMEM((4, 4 * rows, width), BF16),
            pltpu.VMEM((2, 2, rows, width), BF16),
            pltpu.VMEM((2, 4, rows, width), BF16),
            pltpu.VMEM((2, rows // 2, width), BF16),
            pltpu.VMEM((2, rows, width), BF16),
            pltpu.VMEM((8 * cap, hidden), BF16),
            pltpu.VMEM((2, 2, 8 * cap, 256), F32),
            pltpu.VMEM((2, 8 * cap, tile_of(width)), BF16),
            pltpu.VMEM((2, 4 * cap, 4 * rows), F32),
            pltpu.VMEM((4, 2, 4 * cap, 4 * rows), BF16),
            pltpu.VMEM((4, 2, 4 * rows, 4 * cap), BF16),
            pltpu.VMEM((4, 8 * cap, 128), F32),
            pltpu.VMEM((32, 2, 128), F32),
            pltpu.VMEM((32, 2, 128), F32),
            pltpu.VMEM((128, 128), F32),
            dma((3,)), dma((32,)), dma((32,)), dma((18,)), dma((18,)), dma((16,)), dma((16,)),
            dma((16,)), dma((16,)), dma((12,)), dma((12,)), dma((6,)), dma((6,)),
        ],
        compiler_params=pltpu.CompilerParams(
            collective_id=0, has_side_effects=True, vmem_limit_bytes=67043328
        ),
    )(
        tokens_q, token_scale.T, residual, expert_ids.T, gate_values.T,
        w_gate[0], w_up[0], w_down[0],
    )
    new_residual, next_q, next_scale = pl.pallas_call(
        norm_kernel,
        out_shape=(
            jax.ShapeDtypeStruct((rows, width), BF16),
            jax.ShapeDtypeStruct((rows, width), BF16),
            jax.ShapeDtypeStruct((blocks, rows), F32),
        ),
        in_specs=[vmem] * 2,
        out_specs=(vmem, vmem, vmem),
        scratch_shapes=[pltpu.VMEM((128, 128), F32)],
    )(mixed, norm_gain.reshape(blocks, width // blocks))
    return new_residual, next_q, next_scale.T


def solution(mesh):
    rows = P(("dp", "ep"), None)
    weight = P("ep", None, None)
    return jax.shard_map(
        per_device,
        mesh=mesh,
        in_specs=(rows, rows, rows, rows, rows, weight, weight, weight, P()),
        out_specs=(rows, rows, rows),
        check_vma=False,
    )
```

time: 137 us -> 106 us (0.77)
  Pallas kernels: 125 us -> 105 us
  local copies, waits for them, and re-layouts: 10.6 us -> 0 us
    pallas_call x1 -> x2, Pallas kernels: 125 us -> 105 us  [the longest x1 102 us: per_device(): pl.pallas_call(functools.partial(kernel, cap), out_shape=jax.ShapeDtypeSt...]
    unnamed x5 -> x0, local copies, waits for them, and re-layouts: 7.81 us -> none
    pallas_call x1 -> x0, local copies, waits for them, and re-layouts: 1.44 us -> none  [per_device(): pl.pallas_call(functools.partial(kernel, cap), out_shape=(jax.ShapeDtypeS...]
where the time goes in v2:
time: 106 us
  Pallas kernels  105 us (99%)
    pallas_call x1, Pallas kernels, per_device(): pl.pallas_call(functools.partial(kernel, cap), out_shape=jax.ShapeDtypeSt...  102 us
    pallas_call x1, Pallas kernels, per_device(): pl.pallas_call(norm_kernel, out_shape=(jax.ShapeDtypeStruct((rows, width)...  3.03 us

profile of v2, /device:TPU:0, one launch (start us, length us, event | category | flops | bytes accessed | tf_op | source)
XLA Modules:
  0.0 106.1 jit_solution(9038983091649684474)
XLA Ops:
  0.6 102.4 %shard_map.112.mixed_ref = f32[64,3584]{1,0:T(8,128)} custom-call(bf16[64,3584]{1,0:T(8,128)(2,1)} %tq.1, f32[28,64]{1,0:T(8,128)} %bitcast.11, bf16[64,3584]{1,0:T(8,128)(2,1)} %res.1, s32[8,64]{1,0:T(8,128)} %bitcast.13, f32[8,64]{1,0:T(8,128)} %bitcast.14, bf16[3584,1024]{1,0:T(8,128)(2,1)} %bitcast.8, bf16[3584,1024]{1,0:T(8,128)(2,1)} %bitcast.9, ...), custom_call_target="tpu_custom_call" | custom-call | tf_op jit(solution)/shard_map/pallas_call | solution.py:462
  103.0 3.0 %shard_map.113 = (bf16[64,3584]{1,0:T(8,128)(2,1)}, bf16[64,3584]{1,0:T(8,128)(2,1)}, f32[28,64]{1,0:T(8,128)}) custom-call(f32[64,3584]{1,0:T(8,128)} %shard_map.112.mixed_ref, f32[28,128]{1,0:T(8,128)} %bitcast.12), custom_call_target="tpu_custom_call" | custom-call | tf_op jit(solution)/shard_map/pallas_call | solution.py:497

commit v3 on v2

--- a/solution.py
+++ b/solution.py
@@ -13,7 +13,7 @@
 
 BATCHES = (
     ((0, 0), (0, 1), (0, 3), (0, 2)),
-    ((1, 0), (3, 1), (1, 3), (2, 0)),
+    ((2, 0), (1, 0), (3, 1), (1, 3)),
     ((2, 2), (2, 3), (2, 1), (3, 0)),
     ((3, 2), (1, 1), (1, 2), (3, 3)),
 )
@@ -90,20 +90,6 @@
     for n in range(width // qb):
         block = tq[:, n * qb:(n + 1) * qb].astype(F32) * scales[:, n:n + 1]
         XO[0, 2, lo:lo + rows, n * qb:(n + 1) * qb] = block.astype(BF16)
-
-    expert = lax.broadcasted_iota(jnp.int32, (32, rows), 0)
-    gates = jnp.zeros((32, rows), F32)
-    for k in range(ids.shape[0]):
-        gates = gates + jnp.where(ids[k:k + 1, :] == expert, gv[k:k + 1, :], 0.0)
-    before = (
-        lax.broadcasted_iota(jnp.int32, (rows, rows), 0) < lax.broadcasted_iota(jnp.int32, (rows, rows), 1)
-    ).astype(F32).astype(BF16)
-    rank = dot((gates > 0.0).astype(F32).astype(BF16), before)
-    TL[...] = jnp.zeros_like(TL)
-    for e in range(32):
-        TL[e, 0:1, 0:rows] = gates[e:e + 1, :]
-        TL[e, 1:2, 0:rows] = rank[e:e + 1, :]
-    PF[...] = jnp.zeros_like(PF)
 
     pl.semaphore_wait(barrier, 31)
 
@@ -146,6 +132,18 @@
     ag[("a", "1t")].start()
     dd[(0, 0)].start()
 
+    expert = lax.broadcasted_iota(jnp.int32, (32, rows), 0)
+    gates = jnp.zeros((32, rows), F32)
+    for k in range(ids.shape[0]):
+        gates = gates + jnp.where(ids[k:k + 1, :] == expert, gv[k:k + 1, :], 0.0)
+    before = (
+        lax.broadcasted_iota(jnp.int32, (rows, rows), 0) < lax.broadcasted_iota(jnp.int32, (rows, rows), 1)
+    ).astype(F32).astype(BF16)
+    rank = dot((gates > 0.0).astype(F32).astype(BF16), before)
+    TL[...] = jnp.zeros_like(TL)
+    for e in range(32):
+        TL[e, 0:1, 0:rows] = gates[e:e + 1, :]
+        TL[e, 1:2, 0:rows] = rank[e:e + 1, :]
     tables = []
     for s in range(2):
         for (db, da), (i, j) in PLACE.items():
@@ -157,6 +155,7 @@
             c.start()
             tables.append(c)
     T[0] = TL[ep]
+    PF[...] = jnp.zeros_like(PF)
 
     def arrived(db, da):
         ag[(db, da)].wait_recv()
@@ -215,41 +214,35 @@
 
     def gate_up(i):
         def products(n):
-            cols = pl.ds(pl.multiple_of(n * htile, htile), htile)
+            cols = slice(n * htile, (n + 1) * htile)
             GU[n % 2, 0] = dot(XO[0, HOLD[i]], WG[:, cols])
             GU[n % 2, 1] = dot(XO[0, HOLD[i]], WU[:, cols])
 
         def activate(n):
-            cols = pl.ds(pl.multiple_of(n * htile, htile), htile)
+            cols = slice(n * htile, (n + 1) * htile)
             g = GU[n % 2, 0]
             H[:, cols] = (g / (1.0 + jnp.exp(-g)) * GU[n % 2, 1]).astype(BF16)
 
-        def step(n, carry):
-            activate(n - 1)
+        for n in range(hidden // htile):
             products(n)
-            return carry
-
-        products(0)
-        lax.fori_loop(1, hidden // htile, step, 0)
+            if n > 0:
+                activate(n - 1)
         activate(hidden // htile - 1)
 
     def down(i):
         def part(n):
-            cols = pl.ds(pl.multiple_of(n * tile, tile), tile)
+            cols = slice(n * tile, (n + 1) * tile)
             PV[n % 2] = (dot(H[...], WD[:, cols]) * GS[i, :, 0:1]).astype(BF16)
 
         def spread(n):
-            cols = pl.ds(pl.multiple_of(n * tile, tile), tile)
+            cols = slice(n * tile, (n + 1) * tile)
             for s in range(2):
                 XO[s, i, :, cols] = dot(PT[i, s], PV[n % 2, slots * s:slots * (s + 1)]).astype(BF16)
 
-        def step(n, carry):
-            spread(n - 1)
+        for n in range(width // tile):
             part(n)
-            return carry
-
-        part(0)
-        lax.fori_loop(1, width // tile, step, 0)
+            if n > 0:
+                spread(n - 1)
         spread(width // tile - 1)
 
     step_rows = 16
@@ -290,8 +283,13 @@
         r1_move(("f", 0, n), xout(2, far[0][n]), RF.at[0, n], plus_b)
         r1_move(("f", 1, n), xout(2, far[1][n]), RF.at[1, n], minus_b)
     for da in range(4):
-        r1_move(("n", 0, da), xout(1, da), RN.at[0, da], plus_b)
-        r1_move(("n", 1, da), xout(3, da), RN.at[1, da], minus_b)
+        for sign, db, who in ((0, 1, plus_b), (1, 3, minus_b)):
+            if (sign, da) in ((0, 1), (1, 3)):
+                for part in ((low, top), (top, low))[sign]:
+                    name = ("n", sign, da, "l" if part is low else "t")
+                    r1_move(name, xout(db, da).at[part, :], RN.at[sign, da].at[part, :], who)
+            else:
+                r1_move(("n", sign, da), xout(db, da), RN.at[sign, da], who)
 
     def sent(i):
         for c in leaving[i]:
@@ -302,6 +300,14 @@
         r1[("f", sign, n)].wait_recv()
         merge(db, da, RF.at[sign, n])
         r1[("n", sign, da)].start()
+
+    def pass_on_halves(sign):
+        db, da = (1, 3)[sign], far[sign][1]
+        r1[("f", sign, 1)].wait_recv()
+        swap[(db, da)].wait_recv()
+        for name, part in ((("l", low), ("t", top)), (("t", top), ("l", low)))[sign]:
+            add_into(xout(db, da).at[part, :], part_of(db, da).at[part, :], RF.at[sign, 1].at[part, :])
+            r1[("n", sign, da, name)].start()
 
     def send_far(sign, n):
         merge(2, far[sign][n])
@@ -331,10 +337,6 @@
             arrived(3, 3)
             arrived(2, 3)
         elif i == 2:
-            send_near(0, 0)
-            send_near(1, 1)
-            send_near(0, 3)
-            send_far(1, 0)
             arrived(3, 2)
             arrived(1, 1)
         elif i == 3:
@@ -352,12 +354,16 @@
             ag[(1, 1)].start()
             arrived(2, 0)
         elif i == 1:
+            send_far(1, 0)
+            send_near(0, 0)
+            send_near(1, 1)
+            send_near(0, 3)
             arrived(2, 1)
             arrived(2, 2)
     send_near(1, 2)
     pass_on(0, 0)
-    pass_on(1, 1)
-    pass_on(0, 1)
+    pass_on_halves(1)
+    pass_on_halves(0)
 
     def collect(da):
         r1[("n", 0, da)].wait_recv()
@@ -375,15 +381,26 @@
     collect(2)
     r2[0].start()
     r2[1].start()
-    collect(1)
+
+    def collect_half(da, name, part, *more):
+        sign = 0 if da == 1 else 1
+        r1[("n", sign, da, name)].wait_recv()
+        rest = [part_of(0, da), RN.at[0, da], RN.at[1, da]]
+        add_into(xout(0, da).at[part, :], *[x.at[part, :] for x in rest], *more)
+
+    swap[(0, 1)].wait_recv()
+    swap[(0, 3)].wait_recv()
+    r1[("n", 1, 1)].wait_recv()
+    r1[("n", 0, 3)].wait_recv()
+    collect_half(1, "l", low)
     r2[2].start()
-    collect(3)
+    collect_half(3, "t", top)
     r2[3].start()
     r2[0].wait_recv()
-    add_into(xout(0, 1).at[top, :], QF.at[0])
+    collect_half(1, "t", top, QF.at[0])
     r2[4].start()
     r2[1].wait_recv()
-    add_into(xout(0, 3).at[low, :], QF.at[1])
+    collect_half(3, "l", low, QF.at[1])
     r2[5].start()
 
     r1[("n", 0, 0)].wait_recv()
@@ -430,8 +447,8 @@
     step_rows = 16
     SQ[...] = jnp.zeros_like(SQ)
 
-    def step(n, carry):
-        r = pl.ds(pl.multiple_of(n * step_rows, step_rows), step_rows)
+    for n in range(rows // step_rows):
+        r = slice(n * step_rows, (n + 1) * step_rows)
         mixed = mixed_ref[r, :]
         nr_out[r, :] = mixed.astype(BF16)
         scaled = lax.rsqrt(jnp.mean(mixed * mixed, axis=-1, keepdims=True) + 1e-06)
@@ -440,12 +457,9 @@
         for b in range(width // qb):
             block = mixed[:, b * qb:(b + 1) * qb] * scaled * gain[b:b + 1, :]
             scale = (jnp.max(jnp.abs(block), axis=-1, keepdims=True) + 1e-06) / 448.0
-            nq_out[r, b * qb:(b + 1) * qb] = (block / scale).astype(BF16)
+            nq_out[r, b * qb:(b + 1) * qb] = (block * (1.0 / scale)).astype(BF16)
             scales = jnp.where(lanes == b, scale, scales)
         SQ[r, :] = scales
-        return carry
-
-    lax.fori_loop(0, rows // step_rows, step, 0)
     ns_out[...] = SQ[...].T[0:width // qb, 0:rows]
 
 
@@ -485,7 +499,7 @@
             pltpu.VMEM((32, 2, 128), F32),
             pltpu.VMEM((128, 128), F32),
             dma((3,)), dma((32,)), dma((32,)), dma((18,)), dma((18,)), dma((16,)), dma((16,)),
-            dma((16,)), dma((16,)), dma((12,)), dma((12,)), dma((6,)), dma((6,)),
+            dma((16,)), dma((16,)), dma((14,)), dma((14,)), dma((6,)), dma((6,)),
         ],
         compiler_params=pltpu.CompilerParams(
             collective_id=0, has_side_effects=True, vmem_limit_bytes=67043328

time: 106 us -> 99.8 us (0.942)
  Pallas kernels: 105 us -> 98.7 us
    pallas_call x1, Pallas kernels: 102 us -> 96.2 us  [per_device(): pl.pallas_call(functools.partial(kernel, cap), out_shape=jax.ShapeDtypeSt...]
where the time goes in v3:
time: 99.8 us; the launch traced here: 99.4 us
  Pallas kernels  98.7 us (99%)
    pallas_call x1, Pallas kernels, per_device(): pl.pallas_call(functools.partial(kernel, cap), out_shape=jax.ShapeDtypeSt...  96.2 us
    pallas_call x1, Pallas kernels, per_device(): pl.pallas_call(norm_kernel, out_shape=(jax.ShapeDtypeStruct((rows, width)...  2.54 us

profile of v3, /device:TPU:0, one launch (start us, length us, event | category | flops | bytes accessed | tf_op | source)
XLA Modules:
  0.0 99.4 jit_solution(6775436529953970840)
XLA Ops:
  0.6 96.2 %shard_map.112.mixed_ref = f32[64,3584]{1,0:T(8,128)} custom-call(bf16[64,3584]{1,0:T(8,128)(2,1)} %tq.1, f32[28,64]{1,0:T(8,128)} %bitcast.11, bf16[64,3584]{1,0:T(8,128)(2,1)} %res.1, s32[8,64]{1,0:T(8,128)} %bitcast.13, f32[8,64]{1,0:T(8,128)} %bitcast.14, bf16[3584,1024]{1,0:T(8,128)(2,1)} %bitcast.8, bf16[3584,1024]{1,0:T(8,128)(2,1)} %bitcast.9, ...), custom_call_target="tpu_custom_call" | custom-call | tf_op jit(solution)/shard_map/pallas_call | solution.py:476
  96.8 2.5 %shard_map.113 = (bf16[64,3584]{1,0:T(8,128)(2,1)}, bf16[64,3584]{1,0:T(8,128)(2,1)}, f32[28,64]{1,0:T(8,128)}) custom-call(f32[64,3584]{1,0:T(8,128)} %shard_map.112.mixed_ref, f32[28,128]{1,0:T(8,128)} %bitcast.12), custom_call_target="tpu_custom_call" | custom-call | tf_op jit(solution)/shard_map/pallas_call | solution.py:511

commit v4 on v3

--- a/solution.py
+++ b/solution.py
@@ -354,12 +354,12 @@
             ag[(1, 1)].start()
             arrived(2, 0)
         elif i == 1:
+            arrived(2, 1)
+            arrived(2, 2)
             send_far(1, 0)
             send_near(0, 0)
             send_near(1, 1)
             send_near(0, 3)
-            arrived(2, 1)
-            arrived(2, 2)
     send_near(1, 2)
     pass_on(0, 0)
     pass_on_halves(1)

time: 99.8 us -> 99.8 us (level)
  no operation moved by 1% of the time
where the time goes in v4:
time: 99.8 us; the launch traced here: 99.6 us
  Pallas kernels  99 us (99%)
    pallas_call x1, Pallas kernels, per_device(): pl.pallas_call(functools.partial(kernel, cap), out_shape=jax.ShapeDtypeSt...  96.5 us
    pallas_call x1, Pallas kernels, per_device(): pl.pallas_call(norm_kernel, out_shape=(jax.ShapeDtypeStruct((rows, width)...  2.54 us

profile of v4, /device:TPU:0, one launch (start us, length us, event | category | flops | bytes accessed | tf_op | source)
XLA Modules:
  0.0 99.6 jit_solution(14594406269907986678)
XLA Ops:
  0.6 96.5 %shard_map.112.mixed_ref = f32[64,3584]{1,0:T(8,128)} custom-call(bf16[64,3584]{1,0:T(8,128)(2,1)} %tq.1, f32[28,64]{1,0:T(8,128)} %bitcast.11, bf16[64,3584]{1,0:T(8,128)(2,1)} %res.1, s32[8,64]{1,0:T(8,128)} %bitcast.13, f32[8,64]{1,0:T(8,128)} %bitcast.14, bf16[3584,1024]{1,0:T(8,128)(2,1)} %bitcast.8, bf16[3584,1024]{1,0:T(8,128)(2,1)} %bitcast.9, ...), custom_call_target="tpu_custom_call" | custom-call | tf_op jit(solution)/shard_map/pallas_call | solution.py:476
  97.1 2.5 %shard_map.113 = (bf16[64,3584]{1,0:T(8,128)(2,1)}, bf16[64,3584]{1,0:T(8,128)(2,1)}, f32[28,64]{1,0:T(8,128)}) custom-call(f32[64,3584]{1,0:T(8,128)} %shard_map.112.mixed_ref, f32[28,128]{1,0:T(8,128)} %bitcast.12), custom_call_target="tpu_custom_call" | custom-call | tf_op jit(solution)/shard_map/pallas_call | solution.py:511
